TPU v7x, 8 devices: a whole 2x2x1 slice. The times are simulated.
8 devices in a mesh: dp: 1 (over z), tp2: 2 (over y), tp: 4 (over x, core).
Axes of the slice: x: 2, y: 2, z: 1, core: 2. Of those that a mesh axis runs over, the one named last changes fastest.
Arguments:
- hidden: bfloat16 [1024, 4096], P('dp')
- w_gate: bfloat16 [4096, 11008], P(None, ('tp2', 'tp'))
- w_up: bfloat16 [4096, 11008], P(None, ('tp2', 'tp'))
- w_down: bfloat16 [11008, 4096], P(('tp2', 'tp'))
- norm_gain: float32 [4096], replicated
- w_vocab: bfloat16 [4096, 32000], P(None, ('tp2', 'tp'))
- temperature: float32 [1024], P('dp')
- target_ids: int32 [1024], P('dp')
Outputs:
- output 1: float32 [1024], P('dp')
- output 2: float32 [1024], P('dp')
- output 3: float32 [1024], P('dp')
- output 4: bfloat16 [1024, 32000], P('dp', ('tp2', 'tp'))
All inputs are finite; a program needn't handle non-finite values.
Results may differ from a plain program's by a relative error of at most 0.00376407.
Values are sent between devices in bfloat16 or wider.
A program may use at most 1 GiB of HBM per device.

v0:
```python
import jax
import jax.numpy as jnp
from jax import lax
from jax.sharding import PartitionSpec as P

NORM_EPS = 1e-6


def solution(mesh):
    model_axes = ('tp2', 'tp')
    tp_size = mesh.shape['tp']

    def local_step(hidden, w_gate, w_up, w_down, norm_gain, w_vocab, value_a11, target_ids):
        gate_pre = jnp.dot(hidden, w_gate, preferred_element_type=jnp.float32)
        up_pre = jnp.dot(hidden, w_up, preferred_element_type=jnp.float32)
        hidden_act = (jax.nn.silu(gate_pre) * up_pre).astype(jnp.bfloat16)
        part_out = jnp.dot(hidden_act, w_down, preferred_element_type=jnp.float32).astype(jnp.bfloat16)
        mlp_out = lax.psum(part_out, model_axes)
        resid_sum = hidden.astype(jnp.float32) + mlp_out.astype(jnp.float32)
        inv_rms = lax.rsqrt(jnp.mean(resid_sum * resid_sum, axis=-1, keepdims=True) + NORM_EPS)
        normed = (norm_gain * resid_sum * inv_rms).astype(jnp.bfloat16)
        logits = jnp.dot(normed, w_vocab, preferred_element_type=jnp.float32) / value_a11[:, None]
        shard_cols = logits.shape[1]
        shard_index = lax.axis_index('tp2') * tp_size + lax.axis_index('tp')
        local_max = jnp.max(logits, axis=-1)
        shifted = jnp.exp(logits - local_max[:, None])
        local_sum = jnp.sum(shifted, axis=-1)
        local_moment = jnp.sum(shifted * logits, axis=-1)
        local_ids = target_ids - shard_index * shard_cols
        col_ids = jnp.arange(shard_cols, dtype=jnp.int32)
        local_target = jnp.sum(jnp.where(col_ids[None, :] == local_ids[:, None], logits, 0.0), axis=-1)
        global_max = lax.pmax(local_max, model_axes)
        rescale = jnp.exp(local_max - global_max)
        row_stats = jnp.stack([local_sum * rescale, local_moment * rescale, local_target], axis=0)
        totals = lax.psum(row_stats, model_axes)
        log_norm = global_max + jnp.log(totals[0])
        entropy = log_norm - totals[1] / totals[0]
        target_logp = totals[2] - log_norm
        logprobs = (logits - log_norm[:, None]).astype(jnp.bfloat16)
        return log_norm, entropy, target_logp, logprobs

    return jax.shard_map(
        local_step, mesh=mesh,
        in_specs=(P('dp', None), P(None, model_axes), P(None, model_axes), P(model_axes, None),
                  P(None), P(None, model_axes), P('dp'), P('dp')),
        out_specs=(P('dp'), P('dp'), P('dp'), P('dp', model_axes)),
        check_vma=False)
```

profile of v0, /device:TPU:0, one launch (start us, length us, event | category | flops | bytes accessed | tf_op | source)
XLA Modules:
  0.0 303.6 jit_solution(13222175179679594351)
XLA Ops:
  7.2 0.0 all-reduce.2.cloned.1.call-start
  7.2 0.0 copy-start
  7.2 0.0 copy-start.3
  7.2 18.3 %fusion.8 = f32[1024,1376]{0,1:T(8,128)} fusion(bf16[1024,4096]{1,0:T(8,128)(2,1)} %param.8, bf16[4096,1376]{0,1:T(8,128)(2,1)} %param.9), kind=kOutput, calls=%fused_computation.25 | convolution fusion | flops 11542724608 | bytes 25296896 | tf_op jit(solution)/shard_map/dot_general | solution.py:14
  25.5 0.0 copy-done
  25.6 0.0 copy-done.3
  25.6 15.5 %multiply_convert_fusion.2 = bf16[1024,1376]{0,1:T(8,128)(2,1)} fusion(f32[1024,1376]{0,1:T(8,128)} %fusion.8, bf16[1024,4096]{1,0:T(8,128)(2,1)S(1)} %copy-done, bf16[4096,1376]{0,1:T(8,128)(2,1)S(1)} %copy-done.3), kind=kOutput, calls=%fused_computation.14 | convolution fusion | flops 11551178752 | bytes 28114944 | tf_op jit(solution)/shard_map/dot_general | solution.py:15
  41.0 0.0 copy-start.2
  41.0 19.0 %convolution_convert_fusion = bf16[1024,4096]{1,0:T(8,128)(2,1)} fusion(bf16[1024,1376]{0,1:T(8,128)(2,1)} %multiply_convert_fusion.2, bf16[1376,4096]{1,0:T(8,128)(2,1)} %param.11), kind=kOutput, calls=%fused_computation.13 | convolution fusion | flops 11546918912 | bytes 22478848 | tf_op jit(solution)/shard_map/dot_general | solution.py:17
  60.0 0.0 copy-start.4
  60.0 0.0 copy-start.5
  60.0 0.0 all-reduce.2.cloned.1.call-update
  60.0 0.0 copy-done.2
  60.1 117.6 %all-reduce.2.cloned.1.call-done = bf16[1024,4096]{1,0:T(8,128)(2,1)} async-done(((bf16[1024,4096]{1,0:T(8,128)(2,1)}), bf16[1024,4096]{1,0:T(8,128)(2,1)}) %all-reduce.2.cloned.1.call-update) | async-done | bytes 8388624 | tf_op jit(solution)/shard_map/psum | solution.py:18
  177.7 8.5 %multiply_reduce_fusion = f32[1024]{0:T(1024)S(1)} fusion(bf16[1024,4096]{1,0:T(8,128)(2,1)} %all-reduce.2.cloned.1.call-done, bf16[1024,4096]{1,0:T(8,128)(2,1)} %param.8), kind=kLoop, calls=%fused_computation.1 | loop fusion | flops 20970496 | bytes 16781312 | tf_op jit(solution)/shard_map/reduce_sum | solution.py:20
  186.2 0.0 copy-done.4
  186.2 0.0 copy-done.5
  186.2 45.4 %fusion.7 = (f32[1024]{0:T(1024)S(1)}, f32[1024,4000]{0,1:T(8,128)}) fusion(f32[1024]{0:T(1024)S(1)} %copy-done.5, bf16[4096,4000]{0,1:T(8,128)(2,1)} %param.13, bf16[1024,4096]{1,0:T(8,128)(2,1)} %all-reduce.2.cloned.1.call-done, bf16[1024,4096]{1,0:T(8,128)(2,1)} %param.8, f32[1024]{0:T(1024)S(1)} %add_rsqrt_fusion, f32[4096]{0:T(1024)S(1)} %copy-done.4), kind=kOutput, calls=%fused_computation.24 | convolution fusion | flops 33587789824 | bytes 65957888 | tf_op jit(solution)/shard_map/dot_general | solution.py:22
  231.7 22.3 %pmax.7 = f32[1024]{0:T(1024)S(1)} all-reduce(f32[1024]{0:T(1024)S(1)} %get-tuple-element.14), channel_id=1, replica_groups=mesh['dp'=1,'tp2'=2,'tp'=4] {'tp2','tp'}, use_global_device_ids=true, to_apply=%region_3.4 | all-reduce | flops 1024 | bytes 8192 | tf_op jit(solution)/shard_map/pmax | solution.py:32
  254.0 8.5 %fusion = (f32[1024]{0:T(1024)S(1)}, f32[1024]{0:T(1024)S(1)}, f32[1024]{0:T(1024)S(1)}) fusion(f32[1024,4000]{0,1:T(8,128)} %get-tuple-element.15, f32[1024]{0:T(1024)S(1)} %get-tuple-element.14, s32[1024]{0:T(1024)S(1)} %broadcast_subtract_fusion), kind=kLoop, calls=%fused_computation.8 | loop fusion | flops 28668928 | bytes 16404480 | tf_op jit(solution)/shard_map/reduce_sum | solution.py:27
  262.5 24.0 %psum.15 = f32[3,1024]{1,0:T(4,128)S(1)} all-reduce(f32[3,1024]{1,0:T(4,128)S(1)} %pad_maximum_fusion), channel_id=1, replica_groups=mesh['dp'=1,'tp2'=2,'tp'=4] {'tp2','tp'}, use_global_device_ids=true, to_apply=%region_7.8 | all-reduce | flops 3072 | bytes 24576 | tf_op jit(solution)/shard_map/psum | solution.py:35
  286.5 0.6 fusion.6
  287.1 0.0 copy-start.1
  287.1 9.0 %subtract_convert_fusion = bf16[1024,4000]{0,1:T(8,128)(2,1)} fusion(f32[1024,4000]{0,1:T(8,128)} %get-tuple-element.15, f32[1024]{0:T(1024)S(1)} %get-tuple-element.8), kind=kLoop, calls=%fused_computation.3 | loop fusion | flops 8192000 | bytes 24580096 | tf_op jit(solution)/shard_map/convert_element_type | solution.py:39
  296.1 0.0 copy-done.1
  296.1 0.6 sub.36
  (5 shorter events, 0.1 us)
Async XLA Ops:
  7.2 170.5 %all-reduce.2.cloned.1.call-start = ((), (), s32[]{:S(2)}) async-start(), calls=%async_computation | async-start | bytes 16777216 | tf_op jit(solution)/shard_map/psum | solution.py:18
  7.2 18.3 %copy-start = (bf16[1024,4096]{1,0:T(8,128)(2,1)S(1)}, bf16[1024,4096]{1,0:T(8,128)(2,1)}, u32[]{:S(2)}) copy-start(bf16[1024,4096]{1,0:T(8,128)(2,1)} %param.8) | copy-start | bytes 25165828
  7.2 18.3 %copy-start.3 = (bf16[4096,1376]{0,1:T(8,128)(2,1)S(1)}, bf16[4096,1376]{0,1:T(8,128)(2,1)}, u32[]{:S(2)}) copy-start(bf16[4096,1376]{0,1:T(8,128)(2,1)} %param.10) | copy-start | bytes 33816580
  41.0 19.0 %copy-start.2 = (s32[1024]{0:T(1024)S(1)}, s32[1024]{0:T(1024)}, u32[]{:S(2)}) copy-start(s32[1024]{0:T(1024)} %param.15) | copy-start | bytes 12292
  60.0 126.2 %copy-start.4 = (f32[4096]{0:T(1024)S(1)}, f32[4096]{0:T(1024)}, u32[]{:S(2)}) copy-start(f32[4096]{0:T(1024)} %param.12) | copy-start | bytes 49156
  60.0 126.2 %copy-start.5 = (f32[1024]{0:T(1024)S(1)}, f32[1024]{0:T(1024)}, u32[]{:S(2)}) copy-start(f32[1024]{0:T(1024)} %param.14) | copy-start | bytes 12292
  287.1 9.0 %copy-start.1 = (f32[1024]{0:T(1024)}, f32[1024]{0:T(1024)S(1)}, u32[]{:S(2)}) copy-start(f32[1024]{0:T(1024)S(1)} %get-tuple-element.8) | copy-start | bytes 12292
Sparse Core Ops, SparseCore 0:
  60.2 117.4 all-reduce.1
where the time goes:
time: 304 us
  waiting for transfers between devices  118 us (39%)
  matrix products  98.2 us (32%)
  blocking collectives  46.2 us (15%)
  other arithmetic  27.3 us (9%)
  between operations  14.1 us (5%)
    psum x1, waiting for transfers between devices, local_step(): mlp_out = lax.psum(part_out, model_axes)  118 us
    dot_general x1, matrix products, local_step(): jnp.dot(normed, w_vocab, preferred_element_type=jnp.float32)  45.4 us
    psum x1, blocking collectives, local_step(): totals = lax.psum(row_stats, model_axes)  24 us
    pmax x1, blocking collectives, local_step(): global_max = lax.pmax(local_max, model_axes)  22.3 us
    dot_general x1, matrix products, local_step(): jnp.dot(hidden_act, w_down, preferred_element_type=jnp.float32)  19 us
    dot_general x1, matrix products, local_step(): gate_pre = jnp.dot(hidden, w_gate, preferred_element_type=jnp.float32)  18.3 us
    dot_general x1, matrix products, local_step(): up_pre = jnp.dot(hidden, w_up, preferred_element_type=jnp.float32)  15.5 us
    convert_element_type x1, other arithmetic, local_step(): logprobs = (logits - log_norm[:, None]).astype(jnp.bfloat16)  9.02 us
  transfers between devices with their start and end apart: 1, of which 1 were waited for; matrix products, arithmetic and copies ran while one was open for 0% of the time, Pallas kernels for 0%

commit v1 on v0

v1 whole, which is shorter than its diff:
```python
import jax
import jax.numpy as jnp
from jax import lax
from jax.experimental import pallas as pl
from jax.experimental.pallas import tpu as pltpu
from jax.sharding import PartitionSpec as P

NORM_EPS = 1e-6
ROWS = 256
CHUNKS = 4
D = 4096
FF = 1376
V = 4000
GB = ((0, 512), (512, 512), (1024, 352))
VL = ((2752, 1248), (0, 1024), (1376, 1024), (1024, 352), (2400, 352))
VB = ((2752, 512), (3264, 736), (0, 512), (512, 512), (1376, 512), (1888, 512), (1024, 352), (2400, 352))
f32, bf16 = jnp.float32, jnp.bfloat16
MESH = pl.DeviceIdType.MESH

TABLE = {
    (1, 1, 1): [('E1', 0)],
    (1, 1, 3): [('E2', 0)],
    (1, 2, 1): [('E3', 0), ('E1', 1)],
    (1, 3, 0): [('E4', 0), ('E5', 0)],
    (1, 3, 1): [('E2', 1), ('E1', 2)],
    (1, 3, 3): [('E6', 0), ('E3', 1)],
    (1, 3, 4): [],
    (2, 0, 0): [('E7', 0), ('E2', 2)],
    (2, 0, 1): [('E1', 3)],
    (2, 0, 2): [('E4', 1)],
    (2, 1, 0): [('E5', 1), ('E3', 2), ('E6', 1), ('E4', 2), ('E2', 3), ('E7', 1)],
    (2, 1, 1): [('E5', 2)],
    (2, 1, 3): [('E6', 2), ('E3', 3)],
    (2, 2, 0): [('E7', 2)],
    (2, 2, 2): [('E4', 3), ('E5', 3)],
    (2, 3, 0): [('E6', 3), ('E7', 3)],
}

KD, KB1A, KB1B, KB2, KA1, KA2A, KA2B, KA3A, KA3B, KA3C, KA3D = range(11)


def kernel(hid, wg, wu, wd, gain, wv, temp, tgt, out, stats,
           X, PB, DR, B1, B2, W, rsc, ST, SR,
           ssem, rsem, st_s, st_r, xsem, gsem, vsem, credit):
    dp = lax.axis_index('dp')
    y = lax.axis_index('tp2')
    tpi = lax.axis_index('tp')
    x = tpi // 2
    c = tpi % 2
    me = y * 4 + tpi
    f = x + c * (y - x)
    s = y + c * (x - y)
    partner = (dp, y, x * 2 + (1 - c))
    nbr1 = (dp, y + c * (1 - 2 * y), (x + (1 - c) * (1 - 2 * x)) * 2 + c)
    nbr2 = (dp, y + (1 - c) * (1 - 2 * y), (x + c * (1 - 2 * x)) * 2 + c)
    half = c * 128

    def al(v, n):
        return pl.multiple_of(v, n)

    def q(fp, sp):
        return al((2 * fp + sp) * 32, 32)

    def xload(i):
        return pltpu.make_async_copy(hid.at[pl.ds(i * ROWS, ROWS), :], X.at[pl.ds(i * ROWS, ROWS), :], xsem.at[i])

    def gload(b, k):
        src, base = ((wg, 0), (wu, FF))[k]
        r0, n = GB[b]
        return pltpu.make_async_copy(src.at[pl.ds(r0, n), :], W.at[pl.ds(base + r0, n), :], gsem.at[b, k])

    def vload(t):
        r0, n = VL[t]
        return pltpu.make_async_copy(wv.at[pl.ds(r0, n), :], W.at[pl.ds(r0, n), :], vsem.at[t])

    def remote(src, dst, i, k, dev):
        return pltpu.make_async_remote_copy(src_ref=src, dst_ref=dst, send_sem=ssem.at[i, k], recv_sem=rsem.at[i, k],
                                            device_id=dev, device_id_type=MESH)

    def xrows(i, fp, sp, hb):
        return X.at[pl.ds(al(i * ROWS + hb + q(fp, sp), 32), 32), :]

    def prow(i, fp, sp):
        return PB.at[lax.rem(i, 2), pl.ds(al(half + q(fp, sp), 32), 32), :]

    def copy(i, k):
        sl = lax.rem(i, 2)
        if k == KD:
            return remote(PB.at[sl, pl.ds(al(128 - half, 128), 128), :], DR.at[sl], i, k, partner)
        if k == KB1A:
            return remote(prow(i, 1 - f, 1 - s), B1.at[sl, 0], i, k, nbr1)
        if k == KB1B:
            return remote(prow(i, 1 - f, s), B1.at[sl, 1], i, k, nbr1)
        if k == KB2:
            return remote(prow(i, f, 1 - s), B2.at[sl], i, k, nbr2)
        fp, sp = {KA1: (f, s), KA2A: (f, s), KA3A: (f, s), KA2B: (f, 1 - s), KA3B: (f, 1 - s),
                  KA3C: (1 - f, s), KA3D: (1 - f, 1 - s)}[k]
        dev = {KA1: nbr2, KA2A: nbr1, KA2B: nbr1}.get(k, partner)
        r = xrows(i, fp, sp, half)
        return remote(r, r, i, k, dev)

    def e0(i):
        copy(i, KD).start()

    def e1(i):
        copy(i, KD).wait_recv()
        sl = lax.rem(i, 2)
        for sp, k in ((1 - s, KB1A), (s, KB1B)):
            r0 = q(1 - f, sp)

            def add(t, carry):
                pr = pl.ds(al(half + r0 + t * 16, 16), 16)
                dr = pl.ds(al(r0 + t * 16, 16), 16)
                for cb in range(4):
                    cs = slice(cb * 1024, cb * 1024 + 1024)
                    PB[sl, pr, cs] = (PB[sl, pr, cs].astype(f32) + DR[sl, dr, cs].astype(f32)).astype(bf16)
                return carry

            lax.fori_loop(0, 2, add, 0)
            if k == KB1A and i >= 2:
                pl.semaphore_wait(credit.at[1], 1)
            copy(i, k).start()

    def e2(i):
        copy(i, KB1A).wait_recv()
        sl = lax.rem(i, 2)
        r0 = q(f, 1 - s)

        def add(t, carry):
            pr = pl.ds(al(half + r0 + t * 16, 16), 16)
            dr = pl.ds(al(r0 + t * 16, 16), 16)
            br = pl.ds(al(t * 16, 16), 16)
            for cb in range(4):
                cs = slice(cb * 1024, cb * 1024 + 1024)
                PB[sl, pr, cs] = (PB[sl, pr, cs].astype(f32) + DR[sl, dr, cs].astype(f32)
                                  + B1[sl, 0, br, cs].astype(f32)).astype(bf16)
            return carry

        lax.fori_loop(0, 2, add, 0)
        if i >= 2:
            pl.semaphore_wait(credit.at[2], 1)
        copy(i, KB2).start()

    def e3(i):
        copy(i, KB1B).wait_recv()
        copy(i, KB2).wait_recv()
        sl = lax.rem(i, 2)
        r0 = q(f, s)

        def fin(t, carry):
            pr = pl.ds(al(half + r0 + t * 16, 16), 16)
            dr = pl.ds(al(r0 + t * 16, 16), 16)
            br = pl.ds(al(t * 16, 16), 16)
            xr = pl.ds(al(i * ROWS + half + r0 + t * 16, 16), 16)
            acc = jnp.zeros((16, 128), f32)
            for cb in range(16):
                cs = slice(cb * 256, cb * 256 + 256)
                part = (PB[sl, pr, cs].astype(f32) + DR[sl, dr, cs].astype(f32)
                        + B1[sl, 1, br, cs].astype(f32) + B2[sl, br, cs].astype(f32)).astype(bf16)
                r = X[xr, cs].astype(f32) + part.astype(f32)
                rsc[:, cs] = r
                sq = r * r
                acc = acc + sq[:, :128] + sq[:, 128:]
            ms = jnp.sum(acc, axis=1, keepdims=True) * (1.0 / D)
            inv = lax.rsqrt(ms + NORM_EPS)
            for cb in range(16):
                cs = slice(cb * 256, cb * 256 + 256)
                X[xr, cs] = (gain[:, cs] * rsc[:, cs] * inv).astype(bf16)
            return carry

        lax.fori_loop(0, 2, fin, 0)
        copy(i, KA1).start()
        copy(i, KA2A).start()
        copy(i, KA3A).start()
        if i < 2:
            for n, dev in ((0, partner), (1, nbr1), (2, nbr2)):
                pl.semaphore_signal(credit.at[n], inc=1, device_id=dev, device_id_type=MESH)

    def e4(i):
        copy(i, KA1).wait_recv()
        copy(i, KA2B).start()
        copy(i, KA3B).start()

    def e5(i):
        copy(i, KA2A).wait_recv()
        copy(i, KA3C).start()

    def e6(i):
        copy(i, KA2B).wait_recv()
        copy(i, KA3D).start()

    def e7(i):
        for k in (KA3A, KA3B, KA3C, KA3D):
            copy(i, k).wait_recv()

    events = {'E1': e1, 'E2': e2, 'E3': e3, 'E4': e4, 'E5': e5, 'E6': e6, 'E7': e7}

    def progress(phase, i, b):
        for ck in range(CHUNKS):
            todo = TABLE.get((phase, ck, b), [])
            if todo:
                @pl.when(i == ck)
                def _():
                    for name, cc in todo:
                        events[name](cc)

    xload(0).start()
    for b in range(3):
        for k in range(2):
            gload(b, k).start()

    def dott(w, xv):
        return lax.dot_general(w, xv, (((1,), (1,)), ((), ())), preferred_element_type=f32)

    def phase1(wdv, act, dsem):
        def dload(k):
            cs = pl.ds(2048 * k, 2048)
            return pltpu.make_async_copy(wd.at[:, cs], wdv.at[:, cs], dsem.at[k])

        for k in range(2):
            dload(k).start()
        for i in range(1, CHUNKS):
            xload(i).start()

        bar = pltpu.get_barrier_semaphore()
        for d in range(1, 8):
            o = (me + d) % 8
            pl.semaphore_signal(bar, inc=1, device_id=(dp, o // 4, o % 4), device_id_type=MESH)
        pl.semaphore_wait(bar, 7)

        def chunk(i, carry):
            rows = pl.ds(al(i * ROWS, ROWS), ROWS)
            sl = lax.rem(i, 2)
            xload(i).wait()

            def first(fn):
                pl.when(i == 0)(fn)

            def last(fn):
                pl.when(i == CHUNKS - 1)(fn)

            for b, (r0, n) in enumerate(GB):
                @first
                def _():
                    for k in range(2):
                        gload(b, k).wait()

                progress(1, i, b)
                g = dott(W[r0:r0 + n, :], X[rows, :])
                u = dott(W[FF + r0:FF + r0 + n, :], X[rows, :])
                h = g * jax.nn.sigmoid(g) * u
                act[:, r0:r0 + n] = jnp.transpose(h.astype(bf16))

                @last
                def _():
                    for t in ((), (1, 2), (3, 4))[b]:
                        vload(t).start()

            @first
            def _():
                vload(0).start()

            for b in range(2):
                first(lambda: dload(b).wait())
                progress(1, i, 3 + b)
                if b == 0:
                    @pl.when(i >= 2)
                    def _():
                        for k in (KD, KB1A, KB1B, KB2):
                            copy(i - 2, k).wait_send()

                for n in range(8):
                    cs = slice(2048 * b + 256 * n, 2048 * b + 256 * n + 256)
                    PB[sl, :, cs] = jnp.dot(act[...], wdv[:, cs], preferred_element_type=f32).astype(bf16)

            @pl.when(i >= 2)
            def _():
                pl.semaphore_wait(credit.at[0], 1)

            e0(i)
            return carry

        lax.fori_loop(0, CHUNKS, chunk, 0)

    pl.run_scoped(phase1, pltpu.VMEM((FF, D), bf16), pltpu.VMEM((ROWS, FF), bf16), pltpu.SemaphoreType.DMA((2,)))

    def phase2(L, OS, state, IT, TG, LN, osem):
        sub = lax.broadcasted_iota(jnp.int32, (8, ROWS), 0)

        def stats_block(cur, b):
            groups = [r0 + 8 * g for r0, n in VB[2 * b:2 * b + 2] for g in range(n // 8)]
            ms = [L[cur, r:r + 8, :] for r in groups[:4]]
            for k, r in enumerate(groups[4:]):
                ms[k % 4] = jnp.maximum(ms[k % 4], L[cur, r:r + 8, :])
            m_new = jnp.maximum(jnp.maximum(ms[0], ms[1]), jnp.maximum(ms[2], ms[3]))
            zero = jnp.zeros((8, ROWS), f32)
            ss, ws, ts = [zero] * 2, [zero] * 2, [zero] * 2
            if b > 0:
                m_old = state[0]
                m_new = jnp.maximum(m_new, m_old)
                scale = jnp.exp(m_old - m_new)
                ss[0], ws[0], ts[0] = state[1] * scale, state[2] * scale, state[3]
            tg = TG[...]
            for k, r in enumerate(groups):
                l = L[cur, r:r + 8, :]
                e = jnp.exp(l - m_new)
                ss[k % 2] = ss[k % 2] + e
                ws[k % 2] = ws[k % 2] + e * l
                ts[k % 2] = ts[k % 2] + jnp.where(sub == tg - r, l, 0.0)
            state[0] = m_new
            state[1] = ss[0] + ss[1]
            state[2] = ws[0] + ws[1]
            state[3] = ts[0] + ts[1]

        def final_block(old, b):
            for r0, n in VB[2 * b:2 * b + 2]:
                for r in range(r0, r0 + n, 16):
                    OS[r:r + 16, :] = (L[old, r:r + 16, :] - LN[0:1, :]).astype(bf16)

        def stat_copy(i, d):
            o = (me + d) % 8
            return pltpu.make_async_remote_copy(src_ref=ST.at[i], dst_ref=SR.at[i, me], send_sem=st_s.at[i, d],
                                                recv_sem=st_r.at[i, me],
                                                device_id=(dp, o // 4, o % 4), device_id_type=MESH)

        def stat_wait(i, d):
            o = (me + d) % 8
            return pltpu.make_async_remote_copy(src_ref=ST.at[i], dst_ref=SR.at[i, o], send_sem=st_s.at[i, d],
                                                recv_sem=st_r.at[i, o],
                                                device_id=(dp, o // 4, o % 4), device_id_type=MESH)

        def send_stats(i):
            m = state[0]
            mx = jnp.max(m, axis=0, keepdims=True)
            e = jnp.exp(m - mx)
            row = lax.broadcasted_iota(jnp.int32, (8, ROWS), 0)
            pk = jnp.broadcast_to(mx, (8, ROWS))
            for n in (1, 2, 3):
                v = state[n] * e if n < 3 else state[n]
                pk = jnp.where(row == n, jnp.sum(v, axis=0, keepdims=True), pk)
            ST[i] = pk
            SR[i, me] = pk
            for d in range(1, 8):
                stat_copy(i, d).start()

        def recv_stats(i):
            for d in range(1, 8):
                stat_wait(i, d).wait_recv()
            parts = [SR[i, o] for o in range(8)]
            mg = parts[0][0:1, :]
            for p_ in parts[1:]:
                mg = jnp.maximum(mg, p_[0:1, :])
            sg = wgt = tl = jnp.zeros((1, ROWS), f32)
            for p_ in parts:
                e = jnp.exp(p_[0:1, :] - mg)
                sg = sg + p_[1:2, :] * e
                wgt = wgt + p_[2:3, :] * e
                tl = tl + p_[3:4, :]
            lg = mg + jnp.log(sg)
            cs = pl.ds(al(i * ROWS, ROWS), ROWS)
            stats[0:1, cs] = lg
            stats[1:2, cs] = lg - wgt / sg
            stats[2:3, cs] = tl - lg
            LN[...] = jnp.broadcast_to(lg, (8, ROWS))

        def ocopy(i):
            return pltpu.make_async_copy(OS, out.at[:, pl.ds(al(i * ROWS, ROWS), ROWS)], osem)

        def chunk(j, carry):
            rows = pl.ds(al(j * ROWS, ROWS), ROWS)
            cur, old = lax.rem(j, 2), lax.rem(j + 1, 2)
            cs = pl.ds(al(j * ROWS, ROWS), ROWS)
            IT[...] = jnp.broadcast_to(1.0 / temp[:, cs], (8, ROWS))
            tid = tgt[:, cs] - me * V
            TG[...] = jnp.broadcast_to(tid, (8, ROWS))

            def vblock(b):
                for r0, n in VB[2 * b:2 * b + 2]:
                    L[cur, r0:r0 + n, :] = dott(W[r0:r0 + n, :], X[rows, :]) * IT[0:1, :]

            for b in range(4):
                @pl.when(j == 0)
                def _():
                    for t in ((0,), (1,), (2,), (3, 4))[b]:
                        vload(t).wait()

                progress(2, j, b)
                if b == 2:
                    @pl.when(j >= 2)
                    def _():
                        ocopy(j - 2).wait()

                    @pl.when(j >= 1)
                    def _():
                        recv_stats(j - 1)
                if b >= 1:
                    stats_block(cur, b - 1)
                vblock(b)
                if b >= 2:
                    @pl.when(j >= 1)
                    def _():
                        final_block(old, 2 * b - 4)
                        final_block(old, 2 * b - 3)
            stats_block(cur, 3)
            send_stats(j)

            @pl.when(j >= 1)
            def _():
                ocopy(j - 1).start()

            return carry

        lax.fori_loop(0, CHUNKS, chunk, 0)
        ocopy(CHUNKS - 2).wait()
        recv_stats(CHUNKS - 1)
        for b in range(4):
            final_block((CHUNKS - 1) % 2, b)
        ocopy(CHUNKS - 1).start()
        for i in range(CHUNKS):
            for k in range(11):
                if k > KB2 or i >= 2:
                    copy(i, k).wait_send()
            for d in range(1, 8):
                stat_copy(i, d).wait_send()
        ocopy(CHUNKS - 1).wait()

    pl.run_scoped(phase2, pltpu.VMEM((2, V, ROWS), f32), pltpu.VMEM((V, ROWS), bf16),
                  pltpu.VMEM((4, 8, ROWS), f32), pltpu.VMEM((8, ROWS), f32), pltpu.VMEM((8, ROWS), jnp.int32),
                  pltpu.VMEM((8, ROWS), f32), pltpu.SemaphoreType.DMA)


def solution(mesh):
    model_axes = ('tp2', 'tp')

    def local_step(hidden, w_gate, w_up, w_down, norm_gain, w_vocab, temperature, target_ids):
        n = hidden.shape[0]
        anyspec = pl.BlockSpec(memory_space=pl.ANY)
        vspec = pl.BlockSpec(memory_space=pltpu.VMEM)
        logprobs, stats = pl.pallas_call(
            kernel,
            out_shape=(jax.ShapeDtypeStruct((V, n), bf16), jax.ShapeDtypeStruct((8, n), f32)),
            in_specs=[anyspec, anyspec, anyspec, anyspec, vspec, anyspec, vspec, vspec],
            out_specs=(anyspec, vspec),
            scratch_shapes=[
                pltpu.VMEM((n, D), bf16),
                pltpu.VMEM((2, ROWS, D), bf16),
                pltpu.VMEM((2, ROWS // 2, D), bf16),
                pltpu.VMEM((2, 2, ROWS // 8, D), bf16),
                pltpu.VMEM((2, ROWS // 8, D), bf16),
                pltpu.VMEM((V, D), bf16),
                pltpu.VMEM((16, D), f32),
                pltpu.VMEM((CHUNKS, 8, ROWS), f32),
                pltpu.VMEM((CHUNKS, 8, 8, ROWS), f32),
                pltpu.SemaphoreType.DMA((CHUNKS, 11)),
                pltpu.SemaphoreType.DMA((CHUNKS, 11)),
                pltpu.SemaphoreType.DMA((CHUNKS, 8)),
                pltpu.SemaphoreType.DMA((CHUNKS, 8)),
                pltpu.SemaphoreType.DMA((CHUNKS,)),
                pltpu.SemaphoreType.DMA((3, 2)),
                pltpu.SemaphoreType.DMA((5,)),
                pltpu.SemaphoreType.REGULAR((3,)),
            ],
            compiler_params=pltpu.CompilerParams(collective_id=0, has_side_effects=True, vmem_limit_bytes=67043328),
        )(hidden, w_gate.T, w_up.T, w_down, norm_gain.reshape(1, D), w_vocab.T,
          temperature.reshape(1, n), target_ids.reshape(1, n))
        return stats[0], stats[1], stats[2], logprobs.T

    return jax.shard_map(
        local_step, mesh=mesh,
        in_specs=(P('dp', None), P(None, model_axes), P(None, model_axes), P(model_axes, None),
                  P(None), P(None, model_axes), P('dp'), P('dp')),
        out_specs=(P('dp'), P('dp'), P('dp'), P('dp', model_axes)),
        check_vma=False)
```

time: 304 us -> 133 us (0.44)
  Pallas kernels: 0 us -> 123 us
  waiting for transfers between devices: 118 us -> 0 us
  matrix products: 98.2 us -> 0 us
  blocking collectives: 46.2 us -> 0 us
  other arithmetic: 27.3 us -> 0 us
  between operations: 14.1 us -> 0.64 us
  local copies, waits for them, and re-layouts: 0.03 us -> 9.08 us
    pallas_call x0 -> x1, Pallas kernels: none -> 123 us  [local_step(): pl.pallas_call(kernel, out_shape=(jax.ShapeDtypeStruct((V, n), bf16), jax...]
    psum x1 -> x0, waiting for transfers between devices: 118 us -> none  [local_step(): mlp_out = lax.psum(part_out, model_axes)]
    dot_general x4 -> x0, matrix products: 98.2 us -> none  [the longest x1 45.4 us: local_step(): jnp.dot(normed, w_vocab, preferred_element_type=jnp.float32)]
    psum x1 -> x0, blocking collectives: 24 us -> none  [local_step(): totals = lax.psum(row_stats, model_axes)]
    pmax x1 -> x0, blocking collectives: 22.3 us -> none  [local_step(): global_max = lax.pmax(local_max, model_axes)]
    reduce_sum x2 -> x0, other arithmetic: 17.1 us -> none  [the longest x1 8.53 us: local_step(): jnp.mean(resid_sum * resid_sum, axis=-1, keepdims=True) + NORM_EPS]
    convert_element_type x1 -> x0, other arithmetic: 9.02 us -> none  [local_step(): logprobs = (logits - log_norm[:, None]).astype(jnp.bfloat16)]
    unnamed x12 -> x1, local copies, waits for them, and re-layouts: 0.03 us -> 7.61 us
  transfers between devices with their start and end apart: 1 -> 0, of which waited for: 1 -> 0; matrix products, arithmetic and copies ran while one was open for 0% -> 0% of each run, Pallas kernels for 0% -> 0%
where the time goes in v1:
time: 133 us
  Pallas kernels  123 us (92%)
  local copies, waits for them, and re-layouts  9.08 us (7%)
    pallas_call x1, Pallas kernels, local_step(): pl.pallas_call(kernel, out_shape=(jax.ShapeDtypeStruct((V, n), bf16), jax...  123 us
    unnamed x1, local copies, waits for them, and re-layouts  7.61 us

profile of v1, /device:TPU:0, one launch (start us, length us, event | category | flops | bytes accessed | tf_op | source)
XLA Modules:
  0.0 132.8 jit_solution(15084483679134807556)
XLA Ops:
  0.6 123.1 %shard_map.111 = (bf16[4000,1024]{1,0:T(8,128)(2,1)}, f32[8,1024]{1,0:T(8,128)}) custom-call(bf16[1024,4096]{1,0:T(8,128)(2,1)} %hid.1, bf16[1376,4096]{1,0:T(8,128)(2,1)} %bitcast.11, bf16[1376,4096]{1,0:T(8,128)(2,1)} %bitcast.12, bf16[1376,4096]{1,0:T(8,128)(2,1)} %wd.1, f32[1,4096]{1,0:T(1,128)} %bitcast.14, bf16[4000,4096]{1,0:T(8,128)(2,1)} %bitcast.10, ...), custom_call_target="tpu_custom_call" | custom-call | tf_op jit(solution)/shard_map/pallas_call | solution.py:439
  123.7 1.5 %fusion = (f32[1,1024]{1,0:T(1,128)}, f32[1,1024]{1,0:T(1,128)}, f32[1,1024]{1,0:T(1,128)}) fusion(f32[8,1024]{1,0:T(8,128)} %get-tuple-element.6), kind=kLoop, calls=%fused_computation | loop fusion | bytes 24576 | tf_op jit(solution)/shard_map/slice | solution.py:466
  125.2 7.6 %copy.13 = bf16[1024,4000]{0,1:T(8,128)(2,1)} copy(bf16[1024,4000]{0,1:T(8,128)(2,1)} %bitcast.13) | data formatting | bytes 16384000

commit v2 on v1

--- a/solution.py
+++ b/solution.py
@@ -1,3 +1,5 @@
+import functools
+
 import jax
 import jax.numpy as jnp
 from jax import lax
@@ -11,35 +13,43 @@
 D = 4096
 FF = 1376
 V = 4000
-GB = ((0, 512), (512, 512), (1024, 352))
+GB = ((0, 256), (256, 256), (512, 512), (1024, 352))
 VL = ((2752, 1248), (0, 1024), (1376, 1024), (1024, 352), (2400, 352))
-VB = ((2752, 512), (3264, 736), (0, 512), (512, 512), (1376, 512), (1888, 512), (1024, 352), (2400, 352))
+VB = (((2752, 624), (3376, 624)), ((0, 512), (512, 512)), ((1376, 512), (1888, 512)), ((1024, 352), (2400, 352)))
+VN = (1248, 1024, 1024, 704)
+VR = (((2752, 0, 1248),), ((0, 0, 1024),), ((1376, 0, 1024),), ((1024, 0, 352), (2400, 352, 352)))
 f32, bf16 = jnp.float32, jnp.bfloat16
 MESH = pl.DeviceIdType.MESH
 
+B1B_LATE = False
 TABLE = {
-    (1, 1, 1): [('E1', 0)],
-    (1, 1, 3): [('E2', 0)],
-    (1, 2, 1): [('E3', 0), ('E1', 1)],
-    (1, 3, 0): [('E4', 0), ('E5', 0)],
-    (1, 3, 1): [('E2', 1), ('E1', 2)],
-    (1, 3, 3): [('E6', 0), ('E3', 1)],
-    (1, 3, 4): [],
-    (2, 0, 0): [('E7', 0), ('E2', 2)],
-    (2, 0, 1): [('E1', 3)],
-    (2, 0, 2): [('E4', 1)],
-    (2, 1, 0): [('E5', 1), ('E3', 2), ('E6', 1), ('E4', 2), ('E2', 3), ('E7', 1)],
-    (2, 1, 1): [('E5', 2)],
-    (2, 1, 3): [('E6', 2), ('E3', 3)],
-    (2, 2, 0): [('E7', 2)],
-    (2, 2, 2): [('E4', 3), ('E5', 3)],
-    (2, 3, 0): [('E6', 3), ('E7', 3)],
+    (1, 1, 0): [('E1a', 0)],
+    (1, 1, 2): [('E1b', 0)],
+    (2, 1, 0): [('E2a', 0)],
+    (2, 1, 1): [('E2b', 0), ('E1a', 1)],
+    (1, 2, 0): [('E3', 0)],
+    (1, 2, 2): [('E1b', 1)],
+    (1, 2, 3): [('E2a', 1)],
+    (2, 2, 1): [('E4', 0)],
+    (1, 3, 1): [('E1a', 2), ('E2b', 1)],
+    (1, 3, 3): [('E3', 1), ('E5', 0)],
+    (2, 3, 1): [('E2a', 2), ('E6', 0), ('E1b', 2), ('E7', 0)],
+    (3, 0, 1): [('E4', 1)],
+    (3, 0, 2): [('E2b', 2), ('E5', 1), ('E1a', 3)],
+    (3, 0, 3): [('E1b', 3), ('E3', 2)],
+    (3, 1, 0): [('E6', 1), ('E7', 1)],
+    (3, 1, 1): [('E2a', 3)],
+    (3, 1, 2): [('E4', 2), ('E2b', 3)],
+    (3, 2, 0): [('E5', 2), ('E3', 3), ('E6', 2), ('E7', 2)],
+    (3, 2, 2): [('E4', 3), ('E5', 3)],
+    (3, 3, 0): [('E6', 3), ('E7', 3)],
 }
 
-KD, KB1A, KB1B, KB2, KA1, KA2A, KA2B, KA3A, KA3B, KA3C, KA3D = range(11)
-
-
-def kernel(hid, wg, wu, wd, gain, wv, temp, tgt, out, stats,
+KD, KB1A, KB1B, KB2, KA1, KA2A, KA2B, KA3A, KA3B, KA3C, KA3D = 0, 2, 4, 6, 8, 9, 10, 11, 12, 13, 14
+NK = 15
+
+
+def kernel(hid, wg, wu, wd, gain, wv, temp, tgt, out, last_l, stats,
            X, PB, DR, B1, B2, W, rsc, ST, SR,
            ssem, rsem, st_s, st_r, xsem, gsem, vsem, credit):
     dp = lax.axis_index('dp')
@@ -80,30 +90,29 @@
     def xrows(i, fp, sp, hb):
         return X.at[pl.ds(al(i * ROWS + hb + q(fp, sp), 32), 32), :]
 
-    def prow(i, fp, sp):
-        return PB.at[lax.rem(i, 2), pl.ds(al(half + q(fp, sp), 32), 32), :]
+    def prow(i, fp, sp, cs):
+        return PB.at[lax.rem(i, 2), pl.ds(al(half + q(fp, sp), 32), 32), cs]
 
     def copy(i, k):
         sl = lax.rem(i, 2)
-        if k == KD:
-            return remote(PB.at[sl, pl.ds(al(128 - half, 128), 128), :], DR.at[sl], i, k, partner)
-        if k == KB1A:
-            return remote(prow(i, 1 - f, 1 - s), B1.at[sl, 0], i, k, nbr1)
-        if k == KB1B:
-            return remote(prow(i, 1 - f, s), B1.at[sl, 1], i, k, nbr1)
-        if k == KB2:
-            return remote(prow(i, f, 1 - s), B2.at[sl], i, k, nbr2)
+        if k < KA1:
+            kind = k - k % 2
+            cs = pl.ds(2048 * (k % 2), 2048)
+            if kind == KD:
+                return remote(PB.at[sl, pl.ds(al(128 - half, 128), 128), cs], DR.at[sl, :, cs], i, k, partner)
+            if kind == KB1A:
+                return remote(prow(i, 1 - f, 1 - s, cs), B1.at[sl, 0, :, cs], i, k, nbr1)
+            if kind == KB1B:
+                return remote(prow(i, 1 - f, s, cs), B1.at[sl, 1, :, cs], i, k, nbr1)
+            return remote(prow(i, f, 1 - s, cs), B2.at[sl, :, cs], i, k, nbr2)
         fp, sp = {KA1: (f, s), KA2A: (f, s), KA3A: (f, s), KA2B: (f, 1 - s), KA3B: (f, 1 - s),
                   KA3C: (1 - f, s), KA3D: (1 - f, 1 - s)}[k]
         dev = {KA1: nbr2, KA2A: nbr1, KA2B: nbr1}.get(k, partner)
         r = xrows(i, fp, sp, half)
         return remote(r, r, i, k, dev)
 
-    def e0(i):
-        copy(i, KD).start()
-
-    def e1(i):
-        copy(i, KD).wait_recv()
+    def e1(i, h):
+        copy(i, KD + h).wait_recv()
         sl = lax.rem(i, 2)
         for sp, k in ((1 - s, KB1A), (s, KB1B)):
             r0 = q(1 - f, sp)
@@ -111,18 +120,19 @@
             def add(t, carry):
                 pr = pl.ds(al(half + r0 + t * 16, 16), 16)
                 dr = pl.ds(al(r0 + t * 16, 16), 16)
-                for cb in range(4):
-                    cs = slice(cb * 1024, cb * 1024 + 1024)
+                for cb in range(2):
+                    cs = slice(2048 * h + cb * 1024, 2048 * h + cb * 1024 + 1024)
                     PB[sl, pr, cs] = (PB[sl, pr, cs].astype(f32) + DR[sl, dr, cs].astype(f32)).astype(bf16)
                 return carry
 
             lax.fori_loop(0, 2, add, 0)
-            if k == KB1A and i >= 2:
+            if k == KB1A and i >= 2 and h == 0:
                 pl.semaphore_wait(credit.at[1], 1)
-            copy(i, k).start()
-
-    def e2(i):
-        copy(i, KB1A).wait_recv()
+            if k == KB1A or not B1B_LATE:
+                copy(i, k + h).start()
+
+    def e2(i, h):
+        copy(i, KB1A + h).wait_recv()
         sl = lax.rem(i, 2)
         r0 = q(f, 1 - s)
 
@@ -130,20 +140,23 @@
             pr = pl.ds(al(half + r0 + t * 16, 16), 16)
             dr = pl.ds(al(r0 + t * 16, 16), 16)
             br = pl.ds(al(t * 16, 16), 16)
-            for cb in range(4):
-                cs = slice(cb * 1024, cb * 1024 + 1024)
+            for cb in range(2):
+                cs = slice(2048 * h + cb * 1024, 2048 * h + cb * 1024 + 1024)
                 PB[sl, pr, cs] = (PB[sl, pr, cs].astype(f32) + DR[sl, dr, cs].astype(f32)
                                   + B1[sl, 0, br, cs].astype(f32)).astype(bf16)
             return carry
 
         lax.fori_loop(0, 2, add, 0)
-        if i >= 2:
+        if i >= 2 and h == 0:
             pl.semaphore_wait(credit.at[2], 1)
-        copy(i, KB2).start()
+        copy(i, KB2 + h).start()
+        if B1B_LATE:
+            copy(i, KB1B + h).start()
 
     def e3(i):
-        copy(i, KB1B).wait_recv()
-        copy(i, KB2).wait_recv()
+        for h in range(2):
+            copy(i, KB1B + h).wait_recv()
+            copy(i, KB2 + h).wait_recv()
         sl = lax.rem(i, 2)
         r0 = q(f, s)
 
@@ -193,7 +206,10 @@
         for k in (KA3A, KA3B, KA3C, KA3D):
             copy(i, k).wait_recv()
 
-    events = {'E1': e1, 'E2': e2, 'E3': e3, 'E4': e4, 'E5': e5, 'E6': e6, 'E7': e7}
+    events = {'E3': e3, 'E4': e4, 'E5': e5, 'E6': e6, 'E7': e7}
+    for h_, n_ in ((0, 'a'), (1, 'b')):
+        events['E1' + n_] = functools.partial(e1, h=h_)
+        events['E2' + n_] = functools.partial(e2, h=h_)
 
     def progress(phase, i, b):
         for ck in range(CHUNKS):
@@ -205,7 +221,7 @@
                         events[name](cc)
 
     xload(0).start()
-    for b in range(3):
+    for b in range(4):
         for k in range(2):
             gload(b, k).start()
 
@@ -253,7 +269,7 @@
 
                 @last
                 def _():
-                    for t in ((), (1, 2), (3, 4))[b]:
+                    for t in ((), (), (1, 2), (3, 4))[b]:
                         vload(t).start()
 
             @first
@@ -262,36 +278,35 @@
 
             for b in range(2):
                 first(lambda: dload(b).wait())
-                progress(1, i, 3 + b)
+                progress(2, i, b)
                 if b == 0:
                     @pl.when(i >= 2)
                     def _():
-                        for k in (KD, KB1A, KB1B, KB2):
+                        for k in range(KA1):
                             copy(i - 2, k).wait_send()
+                        pl.semaphore_wait(credit.at[0], 1)
 
                 for n in range(8):
                     cs = slice(2048 * b + 256 * n, 2048 * b + 256 * n + 256)
                     PB[sl, :, cs] = jnp.dot(act[...], wdv[:, cs], preferred_element_type=f32).astype(bf16)
 
-            @pl.when(i >= 2)
-            def _():
-                pl.semaphore_wait(credit.at[0], 1)
-
-            e0(i)
+                copy(i, KD + b).start()
+
             return carry
 
         lax.fori_loop(0, CHUNKS, chunk, 0)
 
     pl.run_scoped(phase1, pltpu.VMEM((FF, D), bf16), pltpu.VMEM((ROWS, FF), bf16), pltpu.SemaphoreType.DMA((2,)))
 
-    def phase2(L, OS, state, IT, TG, LN, osem):
+    def phase2(L0, L1, L2, L3, OS, state, IT, TG, LN, osem, lsem):
+        L = (L0, L1, L2, L3)
         sub = lax.broadcasted_iota(jnp.int32, (8, ROWS), 0)
 
         def stats_block(cur, b):
-            groups = [r0 + 8 * g for r0, n in VB[2 * b:2 * b + 2] for g in range(n // 8)]
-            ms = [L[cur, r:r + 8, :] for r in groups[:4]]
-            for k, r in enumerate(groups[4:]):
-                ms[k % 4] = jnp.maximum(ms[k % 4], L[cur, r:r + 8, :])
+            groups = [(lo + k, v + k) for v, lo, n in VR[b] for k in range(0, n, 8)]
+            ms = [L[b][cur, r:r + 8, :] for r, _ in groups[:4]]
+            for k, (r, _) in enumerate(groups[4:]):
+                ms[k % 4] = jnp.maximum(ms[k % 4], L[b][cur, r:r + 8, :])
             m_new = jnp.maximum(jnp.maximum(ms[0], ms[1]), jnp.maximum(ms[2], ms[3]))
             zero = jnp.zeros((8, ROWS), f32)
             ss, ws, ts = [zero] * 2, [zero] * 2, [zero] * 2
@@ -301,21 +316,29 @@
                 scale = jnp.exp(m_old - m_new)
                 ss[0], ws[0], ts[0] = state[1] * scale, state[2] * scale, state[3]
             tg = TG[...]
-            for k, r in enumerate(groups):
-                l = L[cur, r:r + 8, :]
+            for k, (r, v) in enumerate(groups):
+                l = L[b][cur, r:r + 8, :]
                 e = jnp.exp(l - m_new)
                 ss[k % 2] = ss[k % 2] + e
                 ws[k % 2] = ws[k % 2] + e * l
-                ts[k % 2] = ts[k % 2] + jnp.where(sub == tg - r, l, 0.0)
+                ts[k % 2] = ts[k % 2] + jnp.where(sub == tg - v, l, 0.0)
             state[0] = m_new
             state[1] = ss[0] + ss[1]
             state[2] = ws[0] + ws[1]
             state[3] = ts[0] + ts[1]
 
         def final_block(old, b):
-            for r0, n in VB[2 * b:2 * b + 2]:
-                for r in range(r0, r0 + n, 16):
-                    OS[r:r + 16, :] = (L[old, r:r + 16, :] - LN[0:1, :]).astype(bf16)
+            for v, lo, n in VR[b]:
+                for k in range(0, n, 16):
+                    OS[v + k:v + k + 16, :] = (L[b][old, lo + k:lo + k + 16, :] - LN[0:1, :]).astype(bf16)
+
+        def ocopies(i, blocks):
+            return [pltpu.make_async_copy(OS.at[pl.ds(v, n), :], out.at[pl.ds(v, n), pl.ds(al(i * ROWS, ROWS), ROWS)],
+                                          osem.at[b, k]) for b in blocks for k, (v, lo, n) in enumerate(VR[b])]
+
+        def lcopies(b):
+            return [pltpu.make_async_copy(L[b].at[(CHUNKS - 1) % 2, pl.ds(lo, n), :], last_l.at[pl.ds(v, n), :], lsem.at[b, k])
+                    for k, (v, lo, n) in enumerate(VR[b])]
 
         def stat_copy(i, d):
             o = (me + d) % 8
@@ -363,9 +386,6 @@
             stats[2:3, cs] = tl - lg
             LN[...] = jnp.broadcast_to(lg, (8, ROWS))
 
-        def ocopy(i):
-            return pltpu.make_async_copy(OS, out.at[:, pl.ds(al(i * ROWS, ROWS), ROWS)], osem)
-
         def chunk(j, carry):
             rows = pl.ds(al(j * ROWS, ROWS), ROWS)
             cur, old = lax.rem(j, 2), lax.rem(j + 1, 2)
@@ -375,8 +395,10 @@
             TG[...] = jnp.broadcast_to(tid, (8, ROWS))
 
             def vblock(b):
-                for r0, n in VB[2 * b:2 * b + 2]:
-                    L[cur, r0:r0 + n, :] = dott(W[r0:r0 + n, :], X[rows, :]) * IT[0:1, :]
+                lo = 0
+                for r0, n in VB[b]:
+                    L[b][cur, lo:lo + n, :] = dott(W[r0:r0 + n, :], X[rows, :]) * IT[0:1, :]
+                    lo += n
 
             for b in range(4):
                 @pl.when(j == 0)
@@ -384,49 +406,66 @@
                     for t in ((0,), (1,), (2,), (3, 4))[b]:
                         vload(t).wait()
 
-                progress(2, j, b)
+                progress(3, j, b)
                 if b == 2:
                     @pl.when(j >= 2)
                     def _():
-                        ocopy(j - 2).wait()
+                        for cp in ocopies(j - 2, range(4)):
+                            cp.wait()
 
                     @pl.when(j >= 1)
                     def _():
                         recv_stats(j - 1)
+
+                vblock(b)
                 if b >= 1:
                     stats_block(cur, b - 1)
-                vblock(b)
                 if b >= 2:
+                    done = (2 * b - 4, 2 * b - 3)
+                    for d in done:
+                        final_block(old, d)
+
                     @pl.when(j >= 1)
                     def _():
-                        final_block(old, 2 * b - 4)
-                        final_block(old, 2 * b - 3)
+                        for cp in ocopies(j - 1, done):
+                            cp.start()
+
+                @pl.when(j == CHUNKS - 1)
+                def _():
+                    for cp in lcopies(b):
+                        cp.start()
+
             stats_block(cur, 3)
             send_stats(j)
-
-            @pl.when(j >= 1)
-            def _():
-                ocopy(j - 1).start()
-
             return carry
 
         lax.fori_loop(0, CHUNKS, chunk, 0)
-        ocopy(CHUNKS - 2).wait()
+        for i in range(CHUNKS):
+            for k in range(NK):
+                if k >= KA1 or i >= 2:
+                    copy(i, k).wait_send()
+        for cp in ocopies(CHUNKS - 2, range(4)):
+            cp.wait()
+        for b in range(4):
+            for cp in lcopies(b):
+                cp.wait()
         recv_stats(CHUNKS - 1)
-        for b in range(4):
-            final_block((CHUNKS - 1) % 2, b)
-        ocopy(CHUNKS - 1).start()
         for i in range(CHUNKS):
-            for k in range(11):
-                if k > KB2 or i >= 2:
-                    copy(i, k).wait_send()
             for d in range(1, 8):
                 stat_copy(i, d).wait_send()
-        ocopy(CHUNKS - 1).wait()
-
-    pl.run_scoped(phase2, pltpu.VMEM((2, V, ROWS), f32), pltpu.VMEM((V, ROWS), bf16),
+
+    pl.run_scoped(phase2, *[pltpu.VMEM((2, n, ROWS), f32) for n in VN], pltpu.VMEM((V, ROWS), bf16),
                   pltpu.VMEM((4, 8, ROWS), f32), pltpu.VMEM((8, ROWS), f32), pltpu.VMEM((8, ROWS), jnp.int32),
-                  pltpu.VMEM((8, ROWS), f32), pltpu.SemaphoreType.DMA)
+                  pltpu.VMEM((8, ROWS), f32), pltpu.SemaphoreType.DMA((4, 2)), pltpu.SemaphoreType.DMA((4, 2)))
+
+
+def finish(lp_ref, l_ref, st_ref, out_ref, s0, s1, s2):
+    n = lp_ref.shape[1]
+    out_ref[:, :n] = lp_ref[...]
+    out_ref[:, n:] = (l_ref[...] - st_ref[0:1, n:]).astype(bf16)
+    s0[...] = st_ref[0:1, :]
+    s1[...] = st_ref[1:2, :]
+    s2[...] = st_ref[2:3, :]
 
 
 def solution(mesh):
@@ -436,11 +475,12 @@
         n = hidden.shape[0]
         anyspec = pl.BlockSpec(memory_space=pl.ANY)
         vspec = pl.BlockSpec(memory_space=pltpu.VMEM)
-        logprobs, stats = pl.pallas_call(
+        early, last_l, stats = pl.pallas_call(
             kernel,
-            out_shape=(jax.ShapeDtypeStruct((V, n), bf16), jax.ShapeDtypeStruct((8, n), f32)),
+            out_shape=(jax.ShapeDtypeStruct((V, n), bf16), jax.ShapeDtypeStruct((V, ROWS), f32),
+                       jax.ShapeDtypeStruct((8, n), f32)),
             in_specs=[anyspec, anyspec, anyspec, anyspec, vspec, anyspec, vspec, vspec],
-            out_specs=(anyspec, vspec),
+            out_specs=(anyspec, anyspec, vspec),
             scratch_shapes=[
                 pltpu.VMEM((n, D), bf16),
                 pltpu.VMEM((2, ROWS, D), bf16),
@@ -451,19 +491,28 @@
                 pltpu.VMEM((16, D), f32),
                 pltpu.VMEM((CHUNKS, 8, ROWS), f32),
                 pltpu.VMEM((CHUNKS, 8, 8, ROWS), f32),
-                pltpu.SemaphoreType.DMA((CHUNKS, 11)),
-                pltpu.SemaphoreType.DMA((CHUNKS, 11)),
+                pltpu.SemaphoreType.DMA((CHUNKS, NK)),
+                pltpu.SemaphoreType.DMA((CHUNKS, NK)),
                 pltpu.SemaphoreType.DMA((CHUNKS, 8)),
                 pltpu.SemaphoreType.DMA((CHUNKS, 8)),
                 pltpu.SemaphoreType.DMA((CHUNKS,)),
-                pltpu.SemaphoreType.DMA((3, 2)),
+                pltpu.SemaphoreType.DMA((4, 2)),
                 pltpu.SemaphoreType.DMA((5,)),
                 pltpu.SemaphoreType.REGULAR((3,)),
             ],
             compiler_params=pltpu.CompilerParams(collective_id=0, has_side_effects=True, vmem_limit_bytes=67043328),
         )(hidden, w_gate.T, w_up.T, w_down, norm_gain.reshape(1, D), w_vocab.T,
           temperature.reshape(1, n), target_ids.reshape(1, n))
-        return stats[0], stats[1], stats[2], logprobs.T
+        row = pl.BlockSpec((1, n), lambda i: (0, 0))
+        logprobs, s0, s1, s2 = pl.pallas_call(
+            finish,
+            grid=(10,),
+            out_shape=(jax.ShapeDtypeStruct((V, n), bf16),) + (jax.ShapeDtypeStruct((1, n), f32),) * 3,
+            in_specs=[pl.BlockSpec((V // 10, n - ROWS), lambda i: (i, 0)), pl.BlockSpec((V // 10, ROWS), lambda i: (i, 0)),
+                      pl.BlockSpec((8, n), lambda i: (0, 0))],
+            out_specs=(pl.BlockSpec((V // 10, n), lambda i: (i, 0)), row, row, row),
+        )(early, last_l, stats)
+        return s0.reshape(n), s1.reshape(n), s2.reshape(n), logprobs.T
 
     return jax.shard_map(
         local_step, mesh=mesh,

time: 133 us -> 130 us (0.977)
  local copies, waits for them, and re-layouts: 9.08 us -> 0 us
  Pallas kernels: 123 us -> 129 us
    pallas_call x0 -> x1, Pallas kernels: none -> 10.2 us  [local_step(): pl.pallas_call(finish, grid=(10,), out_shape=(jax.ShapeDtypeStruct((V, n)...]
    unnamed x1 -> x0, local copies, waits for them, and re-layouts: 7.61 us -> none
    pallas_call x1, Pallas kernels: 123 us -> 119 us  [local_step(): pl.pallas_call(kernel, out_shape=(jax.ShapeDtypeStruct((V, n), bf16), jax...]
    slice x1 -> x0, local copies, waits for them, and re-layouts: 1.48 us -> none  [local_step(): return (stats[0], stats[1], stats[2], logprobs.T)]
where the time goes in v2:
time: 130 us
  Pallas kernels  129 us (99%)
    pallas_call x1, Pallas kernels, local_step(): pl.pallas_call(kernel, out_shape=(jax.ShapeDtypeStruct((V, n), bf16), jax...  119 us
    pallas_call x1, Pallas kernels, local_step(): pl.pallas_call(finish, grid=(10,), out_shape=(jax.ShapeDtypeStruct((V, n)...  10.2 us

profile of v2, /device:TPU:0, one launch (start us, length us, event | category | flops | bytes accessed | tf_op | source)
XLA Modules:
  0.0 129.9 jit_solution(11568895474228429926)
XLA Ops:
  0.6 119.1 %shard_map.111 = (bf16[4000,1024]{1,0:T(8,128)(2,1)}, f32[4000,256]{1,0:T(8,128)}, f32[8,1024]{1,0:T(8,128)}) custom-call(bf16[1024,4096]{1,0:T(8,128)(2,1)} %hid.1, bf16[1376,4096]{1,0:T(8,128)(2,1)} %bitcast.11, bf16[1376,4096]{1,0:T(8,128)(2,1)} %bitcast.12, bf16[1376,4096]{1,0:T(8,128)(2,1)} %wd.1, f32[1,4096]{1,0:T(1,128)} %bitcast.13, ...), custom_call_target="tpu_custom_call" | custom-call | tf_op jit(solution)/shard_map/pallas_call | solution.py:478
  119.7 10.2 %shard_map.112 = (bf16[4000,1024]{1,0:T(8,128)(2,1)}, f32[1,1024]{1,0:T(1,128)}, f32[1,1024]{1,0:T(1,128)}, f32[1,1024]{1,0:T(1,128)}) custom-call(bf16[4000,1024]{1,0:T(8,128)(2,1)} %get-tuple-element.11.lp_ref, f32[4000,256]{1,0:T(8,128)} %get-tuple-element.12.l_ref, f32[8,1024]{1,0:T(8,128)} %get-tuple-element.13.st_ref), custom_call_target="tpu_custom_call" | custom-call | tf_op jit(solution)/shard_map/pallas_call | solution.py:507
